TPU v7x, 32 devices: a whole 2x2x4 slice. The times are simulated.
32 devices in a mesh: dev: 32 (over z, y, x, core).
Axes of the slice: x: 2, y: 2, z: 4, core: 2. Of those that a mesh axis runs over, the one named last changes fastest.
Arguments:
- pixels: bfloat16 [96, 64, 16], P('dev'), may hold values from -6 to 6
- embed_w: bfloat16 [96, 16, 8192], P('dev'), may hold values from -1.5 to 1.5
- var_embed: bfloat16 [96, 8192], P('dev'), may hold values from -3 to 3
- key_w: bfloat16 [8192, 8192], P('dev'), may hold values from -0.0625 to 0.0625
- query: float32 [8192], replicated, may hold values from -500 to 500
- value_t: bfloat16 [8192, 8192], P('dev'), may hold values from -0.0625 to 0.0625
- out_w: bfloat16 [8192, 8192], P('dev'), may hold values from -0.0625 to 0.0625
Outputs:
- mixed: bfloat16 [64, 8192], P('dev')
All inputs are finite; a program needn't handle non-finite values.
Results may differ from a plain program's by a relative error of at most 0.012.
The roundings to bfloat16 on the way count: a program that leaves them out, or rounds other values in their place, can miss the bound.
Values may be sent and summed in bfloat16 or wider, within the bound.
No kernel may reach another device: no remote copies, remote signals or barrier semaphores. Data moves between devices by JAX's collectives and lax.ppermute only.
A program may use at most 64 MiB of HBM per device.

v0:
```python
import jax
import jax.numpy as jnp
from jax import lax
from jax.sharding import PartitionSpec as P

D = 8192
HEADS = 64
HD = 128
V = 91


def body(pixels, embed_w, var_embed, key_w, query, value_t, out_w):
    group_size = lax.axis_size("dev")
    own_embed = jnp.einsum("vtp,vpd->vtd", pixels, embed_w, preferred_element_type=jnp.float32)
    own_embed = (own_embed + var_embed.astype(jnp.float32)[:, None, :]).astype(jnp.bfloat16)
    grouped = lax.all_to_all(own_embed, "dev", split_axis=1, concat_axis=0, tiled=True)
    key_rows = key_w.shape[0]
    keyq_part = jnp.einsum(
        "dhj,hj->dh",
        key_w.astype(jnp.float32).reshape(key_rows, HEADS, HD),
        query.reshape(HEADS, HD),
        precision=lax.Precision.HIGHEST,
    )
    keyq = lax.all_gather(keyq_part, "dev", axis=0, tiled=True)
    logits = jnp.einsum(
        "vtd,dh->vth", grouped.astype(jnp.float32), keyq, precision=lax.Precision.HIGHEST
    ) / jnp.sqrt(jnp.float32(HD))
    slot = lax.broadcasted_iota(jnp.int32, logits.shape, 0)
    logits = jnp.where(slot < V, logits, -1e30)
    row_max = jnp.max(logits, axis=0, keepdims=True)
    weights = jnp.exp(logits - row_max)
    attn = (weights / jnp.sum(weights, axis=0, keepdims=True)).astype(jnp.bfloat16)
    pooled = jnp.einsum("vth,vtd->thd", attn, grouped, preferred_element_type=jnp.float32).astype(
        jnp.bfloat16
    )
    own_tokens = pooled.shape[0]
    if group_size >= HEADS:
        spread = jnp.repeat(pooled, group_size // HEADS, axis=1)[:, :, None, :]
    else:
        spread = pooled.reshape(own_tokens, group_size, HEADS // group_size, D)
    received = lax.all_to_all(spread, "dev", split_axis=1, concat_axis=0, tiled=True)
    all_tokens = received.shape[0]
    head_share = received.shape[2]
    received = received.reshape(all_tokens, head_share, D)
    columns = value_t.shape[0]
    value_heads = jnp.einsum(
        "thd,hcd->thc",
        received,
        value_t.reshape(head_share, columns // head_share, D),
        preferred_element_type=jnp.float32,
    )
    value_heads = value_heads.reshape(all_tokens, columns).astype(jnp.bfloat16)
    summed = lax.psum_scatter(
        jnp.dot(value_heads, out_w, preferred_element_type=jnp.float32),
        "dev",
        scatter_dimension=0,
        tiled=True,
    )
    return summed.astype(jnp.bfloat16)


def solution(mesh):
    placed = (
        P("dev", None, None),
        P("dev", None, None),
        P("dev", None),
        P("dev", None),
        P(),
        P("dev", None),
        P("dev", None),
    )
    return jax.shard_map(
        body, mesh=mesh, in_specs=placed, out_specs=P("dev", None), check_vma=False
    )
```

profile of v0, /device:TPU:0, one launch (start us, length us, event | category | flops | bytes accessed | tf_op | source)
XLA Modules:
  0.0 285.6 jit_solution(11926075932730230169)
XLA Ops:
  6.5 0.0 copy-start
  6.5 0.9 convert_element_type.26
  7.5 0.2 copy-done
  7.7 1.7 fusion.1
  9.4 4.7 %copy.15 = bf16[3,64,8192]{2,0,1:T(4,128)(2,1)} copy(bf16[3,64,8192]{2,1,0:T(8,128)(2,1)S(1)} %fusion.1) | data formatting | bytes 6291456 | tf_op jit(solution)/shard_map/convert_element_type | solution.py:15
  14.1 7.4 %all-to-all-start = ((bf16[3,64,8192]{2,0,1:T(4,128)(2,1)}), bf16[3,64,8192]{2,0,1:T(4,128)(2,1)}, u32[]{:S(2)}, u32[]{:S(2)}) async-start(bf16[3,64,8192]{2,0,1:T(4,128)(2,1)} %copy.15), calls=%async_computation | async-start | bytes 8388608 | tf_op jit(solution)/shard_map/all_to_all | solution.py:16
  21.6 0.0 copy-start.2
  21.6 0.0 all-gather.2.cloned.1.call-start
  21.6 6.4 %copy.25 = bf16[256,8192]{0,1:T(8,128)(2,1)} copy(bf16[256,8192]{1,0:T(8,128)(2,1)} %param.10) | data formatting | bytes 8388608 | tf_op jit(solution)/shard_map/reshape | solution.py:20
  28.0 0.0 copy-done.2
  28.0 3.9 %fusion.32 = f32[64,1,256]{2,1,0:T(1,128)S(1)} fusion(f32[64,128,1]{1,2,0:T(1,128)S(1)} %bitcast.48, bf16[256,64,128]{0,2,1:T(8,128)(2,1)} %bitcast.44), kind=kOutput, calls=%fused_computation.26 | convolution fusion | flops 25165824 | bytes 4292608 | tf_op jit(solution)/shard_map/dhj,hj->dh/dot_general | solution.py:18
  31.9 0.6 copy.47
  32.5 0.0 all-gather.2.cloned.1.call-update
  32.6 93.2 %all-to-all-done = bf16[3,64,8192]{2,0,1:T(4,128)(2,1)} async-done(((bf16[3,64,8192]{2,0,1:T(4,128)(2,1)}), bf16[3,64,8192]{2,0,1:T(4,128)(2,1)}, u32[]{:S(2)}, u32[]{:S(2)}) %all-to-all-start) | async-done | bytes 3145760 | tf_op jit(solution)/shard_map/all_to_all | solution.py:16
  125.8 7.9 %copy.16 = bf16[3,32,2,8192]{3,2,0,1:T(2,128)(2,1)} copy(bf16[3,32,2,8192]{3,0,2,1:T(4,128)(2,1)} %bitcast) | data formatting | bytes 6291456 | tf_op jit(solution)/shard_map/all_to_all | solution.py:16
  133.7 0.0 all-gather.2.cloned.1.call-done
  133.7 9.0 %fusion.15 = f32[96,2,64]{0,2,1:T(8,128)S(1)} fusion(f32[8192,64]{0,1:T(8,128)} %all-gather.2.cloned.1.call-done, bf16[96,2,8192]{2,1,0:T(2,128)(2,1)} %bitcast.42, pred[96]{0:T(512)(128)(4,1)S(1)} %iota_compare_fusion), kind=kOutput, calls=%fused_computation.13 | convolution fusion | flops 1207984128 | bytes 5292128 | tf_op jit(solution)/shard_map/vtd,dh->vth/dot_general | solution.py:25
  142.7 0.2 fusion.31
  142.9 6.0 %convolution_convert_fusion = bf16[2,64,8192]{2,1,0:T(8,128)(2,1)S(1)} fusion(bf16[96,2,8192]{2,1,0:T(2,128)(2,1)} %bitcast.43, f32[2,64]{1,0:T(2,128)S(1)} %fusion.31, f32[96,2,64]{0,2,1:T(8,128)S(1)} %fusion.15), kind=kOutput, calls=%fused_computation.3 | convolution fusion | flops 202412256 | bytes 5292544 | tf_op jit(solution)/shard_map/vth,vtd->thd/dot_general | solution.py:33
  148.9 2.7 reshape.23
  151.6 6.0 %copy.19 = bf16[2,32,2,8192]{3,2,0,1:T(2,128)(2,1)} copy(bf16[2,32,2,8192]{3,2,1,0:T(2,128)(2,1)} %reshape.23) | data formatting | bytes 4194304 | tf_op jit(solution)/shard_map/reshape | solution.py:40
  157.5 4.1 %all-to-all-start.1 = ((bf16[2,32,2,8192]{3,2,0,1:T(2,128)(2,1)}), bf16[2,32,2,8192]{3,2,0,1:T(2,128)(2,1)S(1)}, u32[]{:S(2)}, u32[]{:S(2)}) async-start(bf16[2,32,2,8192]{3,2,0,1:T(2,128)(2,1)} %copy.19), calls=%async_computation.1 | async-start | bytes 4194304 | tf_op jit(solution)/shard_map/all_to_all | solution.py:41
  161.7 48.7 %all-to-all-done.1 = bf16[2,32,2,8192]{3,2,0,1:T(2,128)(2,1)S(1)} async-done(((bf16[2,32,2,8192]{3,2,0,1:T(2,128)(2,1)}), bf16[2,32,2,8192]{3,2,0,1:T(2,128)(2,1)S(1)}, u32[]{:S(2)}, u32[]{:S(2)}) %all-to-all-start.1) | async-done | bytes 2097184 | tf_op jit(solution)/shard_map/all_to_all | solution.py:41
  210.4 0.0 copy-start.1
  210.4 4.1 %fusion.23 = bf16[2,8,8,128]{3,2,1,0:T(8,128)(2,1)S(1)} fusion(bf16[2,128,8192]{2,1,0:T(8,128)(2,1)} %bitcast.46, bf16[64,2,8192]{2,1,0:T(2,128)(2,1)S(1)} %bitcast.45), kind=kOutput, calls=%fused_computation.15 | convolution fusion | flops 268451840 | bytes 6324224 | tf_op jit(solution)/shard_map/thd,hcd->thc/dot_general | solution.py:46
  214.5 0.0 copy-done.1
  214.5 0.8 fusion.26
  215.4 61.8 %all-reduce.2 = bf16[64,8192]{1,0:T(8,128)(2,1)} all-reduce(f32[64,8192]{1,0:T(8,128)S(1)} %fusion.26), channel_id=2, replica_groups=mesh['dev'=32] {'dev'}, use_global_device_ids=true, to_apply=%region_2.3.clone | all-reduce | flops 524288 | bytes 3145728
  277.2 1.6 dynamic-slice_convert_fusion
  (1 shorter events, 0.0 us)
Async XLA Ops:
  6.5 1.2 copy-start
  14.1 111.7 %all-to-all-start = ((bf16[3,64,8192]{2,0,1:T(4,128)(2,1)}), bf16[3,64,8192]{2,0,1:T(4,128)(2,1)}, u32[]{:S(2)}, u32[]{:S(2)}) async-start(bf16[3,64,8192]{2,0,1:T(4,128)(2,1)} %copy.15), calls=%async_computation | async-start | bytes 8388608 | tf_op jit(solution)/shard_map/all_to_all | solution.py:16
  21.6 6.4 %copy-start.2 = (f32[8192]{0:T(1024)S(1)}, f32[8192]{0:T(1024)}, u32[]{:S(2)}) copy-start(f32[8192]{0:T(1024)} %param.11) | copy-start | bytes 98308
  21.6 112.1 %all-gather.2.cloned.1.call-start = ((), (), s32[]{:S(2)}) async-start(), calls=%async_computation.2 | async-start | bytes 2162688 | tf_op jit(solution)/shard_map/all_gather | solution.py:24
  157.5 52.9 %all-to-all-start.1 = ((bf16[2,32,2,8192]{3,2,0,1:T(2,128)(2,1)}), bf16[2,32,2,8192]{3,2,0,1:T(2,128)(2,1)S(1)}, u32[]{:S(2)}, u32[]{:S(2)}) async-start(bf16[2,32,2,8192]{3,2,0,1:T(2,128)(2,1)} %copy.19), calls=%async_computation.1 | async-start | bytes 4194304 | tf_op jit(solution)/shard_map/all_to_all | solution.py:41
  210.4 4.1 %copy-start.1 = (bf16[256,8192]{1,0:T(8,128)(2,1)S(1)}, bf16[256,8192]{1,0:T(8,128)(2,1)}, u32[]{:S(2)}) copy-start(bf16[256,8192]{1,0:T(8,128)(2,1)} %param.13) | copy-start | bytes 12582916
Sparse Core Ops, SparseCore 0:
  32.7 79.4 all-gather.1
where the time goes:
time: 286 us
  waiting for transfers between devices  142 us (50%)
  blocking collectives  61.8 us (22%)
  local copies, waits for them, and re-layouts  30 us (10%)
  matrix products  25.6 us (9%)
  between operations  13.5 us (5%)
  starting transfers between devices  11.6 us (4%)
    all_to_all x1, waiting for transfers between devices, body(): lax.all_to_all(own_embed, 'dev', split_axis=1, concat_axis=0, tiled=True)  93.2 us
    unnamed x1, blocking collectives  61.8 us
    all_to_all x1, waiting for transfers between devices, body(): lax.all_to_all(spread, 'dev', split_axis=1, concat_axis=0, tiled=True)  48.7 us
    dot_general x1, matrix products, body(): jnp.einsum('vtd,dh->vth', grouped.astype(jnp.float32), keyq, precision=la...  8.99 us
    reshape x2, local copies, waits for them, and re-layouts, body(): spread = pooled.reshape(own_tokens, group_size, HEADS // group_size, D)  8.65 us
    all_to_all x1, local copies, waits for them, and re-layouts, body(): lax.all_to_all(own_embed, 'dev', split_axis=1, concat_axis=0, tiled=True)  7.92 us
    all_to_all x1, starting transfers between devices, body(): lax.all_to_all(own_embed, 'dev', split_axis=1, concat_axis=0, tiled=True)  7.44 us
    reshape x1, local copies, waits for them, and re-layouts, body(): key_w.astype(jnp.float32).reshape(key_rows, HEADS, HD)  6.36 us
  transfers between devices with their start and end apart: 3, of which 2 were waited for; matrix products, arithmetic and copies ran while one was open for 7% of the time, Pallas kernels for 0%

commit v1 on v0

--- a/solution.py
+++ b/solution.py
@@ -59,6 +59,110 @@
     return summed.astype(jnp.bfloat16)
 
 
+def split3(x):
+    hi = lax.reduce_precision(x, 8, 7)
+    rest = x - hi
+    mid = lax.reduce_precision(rest, 8, 7)
+    low = lax.reduce_precision(rest - mid, 8, 7)
+    return [piece.astype(jnp.bfloat16) for piece in (hi, mid, low)]
+
+
+def halves_body(pixels, embed_w, var_embed, key_w, query, value_t, out_w):
+    n_dev = lax.axis_size("dev")
+    half = n_dev // 2
+    me = lax.axis_index("dev")
+    my_half = me // half
+    in_half = [[side * half + i for i in range(half)] for side in range(2)]
+    across = [(i, (i + half) % n_dev) for i in range(n_dev)]
+
+    def exchange(x):
+        return lax.all_to_all(x, "dev", 0, 0, axis_index_groups=in_half, tiled=True)
+
+    own_v, tokens, p_size = pixels.shape
+    width = D // half
+    slots = own_v * n_dev
+    half_heads = HEADS // 2
+    dev_heads = HEADS // n_dev
+
+    w_rows = embed_w.reshape(own_v, p_size, half, width).transpose(2, 0, 1, 3)
+    w_rows = w_rows.reshape(half, own_v * p_size, width)
+    var_rows = var_embed.reshape(own_v, half, width).transpose(1, 0, 2)
+    pix_rows = pixels.transpose(0, 2, 1).reshape(1, -1, width)
+    pix_rows = jnp.broadcast_to(pix_rows, (half,) + pix_rows.shape[1:])
+    packed = jnp.concatenate([w_rows, var_rows, pix_rows], axis=1)
+    n_rows = packed.shape[1]
+    packed = jnp.pad(packed, ((0, 0), (0, -n_rows % 16), (0, 0)))
+    mine = exchange(packed)
+    other = lax.ppermute(mine, "dev", across)
+    first = my_half == 0
+    both = jnp.concatenate(
+        [jnp.where(first, mine, other), jnp.where(first, other, mine)], axis=0
+    )
+    k = own_v * p_size
+    w_all = both[:, :k].reshape(slots, p_size, width)
+    var_all = both[:, k : k + own_v].reshape(slots, width)
+    pix_all = both[:, k + own_v : n_rows].reshape(slots, p_size, tokens)
+    embed = jnp.einsum("vpt,vpd->vtd", pix_all, w_all, preferred_element_type=jnp.float32)
+    embed = (embed + var_all.astype(jnp.float32)[:, None, :]).astype(jnp.bfloat16)
+
+    key_rows = key_w.shape[0]
+    keyq_part = jnp.einsum(
+        "dhj,hj->hd",
+        key_w.astype(jnp.float32).reshape(key_rows, HEADS, HD),
+        query.reshape(HEADS, HD),
+        precision=lax.Precision.HIGHEST,
+    )
+    odd = me % 2
+    low_heads, high_heads = keyq_part[:half_heads], keyq_part[half_heads:]
+    to_same = [(i, i // 2 + half * (i % 2)) for i in range(n_dev)]
+    to_other = [(i, i // 2 + half * (1 - i % 2)) for i in range(n_dev)]
+    got_same = lax.ppermute(jnp.where(odd == 0, low_heads, high_heads), "dev", to_same)
+    got_other = lax.ppermute(jnp.where(odd == 0, high_heads, low_heads), "dev", to_other)
+    keyq = jnp.concatenate(
+        [jnp.where(first, got_same, got_other), jnp.where(first, got_other, got_same)], axis=1
+    )
+    pieces = jnp.concatenate(split3(keyq), axis=0)
+    part = lax.dot_general(
+        pieces,
+        embed.reshape(slots * tokens, width),
+        (((1,), (1,)), ((), ())),
+        preferred_element_type=jnp.float32,
+    )
+    part = part.reshape(3, half_heads, slots * tokens).sum(axis=0)
+    part = part.reshape(half, dev_heads * slots * tokens // 128, 128)
+    logits = exchange(part).reshape(half, dev_heads, slots, tokens).sum(axis=0)
+    logits = logits / jnp.sqrt(jnp.float32(HD))
+    slot = lax.broadcasted_iota(jnp.int32, logits.shape, 1)
+    logits = jnp.where(slot < V, logits, -1e30)
+    row_max = jnp.max(logits, axis=1, keepdims=True)
+    weights = jnp.exp(logits - row_max)
+    attn = (weights / jnp.sum(weights, axis=1, keepdims=True)).astype(jnp.bfloat16)
+    attn = attn.reshape(1, -1, 128)
+    attn = exchange(jnp.broadcast_to(attn, (half,) + attn.shape[1:]))
+    attn = attn.reshape(half_heads, slots, tokens)
+
+    pooled = jnp.einsum("hvt,vtd->thd", attn, embed, preferred_element_type=jnp.float32).astype(
+        jnp.bfloat16
+    )
+    spread = pooled.reshape(tokens, half, dev_heads, width).transpose(1, 2, 0, 3)
+    received = exchange(spread.reshape(half, dev_heads * tokens, width))
+    received = received.reshape(half, dev_heads, tokens, width)
+    columns = value_t.shape[0]
+    value_heads = jnp.einsum(
+        "rhtk,hcrk->thc",
+        received,
+        value_t.reshape(dev_heads, columns // dev_heads, half, width),
+        preferred_element_type=jnp.float32,
+    )
+    value_heads = value_heads.reshape(tokens, columns).astype(jnp.bfloat16)
+    sums = jnp.dot(value_heads, out_w, preferred_element_type=jnp.float32).astype(jnp.bfloat16)
+    sums = lax.all_to_all(
+        sums.reshape(n_dev, -1, 1024), "dev", 0, 0, tiled=True
+    )
+    summed = jnp.sum(sums.astype(jnp.float32), axis=0)
+    return summed.reshape(tokens // n_dev, D).astype(jnp.bfloat16)
+
+
 def solution(mesh):
     placed = (
         P("dev", None, None),
@@ -69,6 +173,8 @@
         P("dev", None),
         P("dev", None),
     )
+    n_dev = mesh.shape["dev"]
+    chosen = halves_body if n_dev % 2 == 0 and HEADS % n_dev == 0 else body
     return jax.shard_map(
-        body, mesh=mesh, in_specs=placed, out_specs=P("dev", None), check_vma=False
+        chosen, mesh=mesh, in_specs=placed, out_specs=P("dev", None), check_vma=False
     )

time: 286 us -> 200 us (0.70)
  waiting for transfers between devices: 142 us -> 88.7 us
  blocking collectives: 61.8 us -> 43 us
  between operations: 13.5 us -> 0.27 us
  local copies, waits for them, and re-layouts: 30 us -> 18 us
  starting transfers between devices: 11.6 us -> 20.6 us
    all_to_all x2 -> x3, waiting for transfers between devices: 142 us -> 52.1 us  [exchange(): return lax.all_to_all(x, 'dev', 0, 0, axis_index_groups=in_half, tiled=True)]
    unnamed x1 -> x0, blocking collectives: 61.8 us -> none
    all_to_all x0 -> x2, blocking collectives: none -> 43 us  [the longest x1 31.2 us: halves_body(): lax.all_to_all(sums.reshape(n_dev, -1, 1024), 'dev', 0, 0, tiled=True)]
    ppermute x0 -> x3, waiting for transfers between devices: none -> 36.6 us  [the longest x1 23.3 us: halves_body(): other = lax.ppermute(mine, 'dev', across)]
    unnamed x6 -> x10, local copies, waits for them, and re-layouts: 0.24 us -> 10 us
    reshape x3 -> x6, local copies, waits for them, and re-layouts: 15 us -> 5.47 us  [the longest x1 2.48 us: halves_body(): pooled.reshape(tokens, half, dev_heads, width).transpose(1, 2, 0, 3)]
    all_to_all x1 -> x0, local copies, waits for them, and re-layouts: 7.92 us -> none  [body(): lax.all_to_all(own_embed, 'dev', split_axis=1, concat_axis=0, tiled=True)]
    ppermute x0 -> x3, starting transfers between devices: none -> 6.58 us  [the longest x1 3.33 us: halves_body(): lax.ppermute(jnp.where(odd == 0, high_heads, low_heads), 'dev', to_other)]
  transfers between devices with their start and end apart: 3 -> 6, of which waited for: 2 -> 5; matrix products, arithmetic and copies ran while one was open for 7% -> 6% of each run, Pallas kernels for 0% -> 0%
where the time goes in v1:
time: 200 us; the launch traced here: 199 us
  waiting for transfers between devices  88.7 us (44%)
  blocking collectives  43 us (22%)
  matrix products  26.7 us (13%)
  starting transfers between devices  20.6 us (10%)
  local copies, waits for them, and re-layouts  18 us (9%)
  other arithmetic  2.02 us (1%)
    all_to_all x3, waiting for transfers between devices, exchange(): return lax.all_to_all(x, 'dev', 0, 0, axis_index_groups=in_half, tiled=True)  52.1 us
    all_to_all x1, blocking collectives, halves_body(): lax.all_to_all(sums.reshape(n_dev, -1, 1024), 'dev', 0, 0, tiled=True)  31.2 us
    ppermute x1, waiting for transfers between devices, halves_body(): other = lax.ppermute(mine, 'dev', across)  23.3 us
    all_to_all x3, starting transfers between devices, exchange(): return lax.all_to_all(x, 'dev', 0, 0, axis_index_groups=in_half, tiled=True)  14 us
    ppermute x1, waiting for transfers between devices, halves_body(): lax.ppermute(jnp.where(odd == 0, high_heads, low_heads), 'dev', to_other)  13.3 us
    all_to_all x1, blocking collectives, exchange(): return lax.all_to_all(x, 'dev', 0, 0, axis_index_groups=in_half, tiled=True)  11.7 us
    unnamed x10, local copies, waits for them, and re-layouts  10 us
    dot_general x1, matrix products, halves_body(): jnp.einsum('hvt,vtd->thd', attn, embed, preferred_element_type=jnp.float32)  9.54 us
  transfers between devices with their start and end apart: 6, of which 5 were waited for; matrix products, arithmetic and copies ran while one was open for 6% of the time, Pallas kernels for 0%

profile of v1, /device:TPU:0, one launch (start us, length us, event | category | flops | bytes accessed | tf_op | source)
XLA Modules:
  0.0 199.2 jit_solution(3742634498450946501)
XLA Ops:
  0.0 0.8 broadcast_in_dim.21
  0.8 1.4 copy.33
  2.3 0.4 copy.20
  2.7 1.1 fusion.25
  3.8 6.3 %all-to-all-start = ((bf16[16,64,512]{2,1,0:T(8,128)(2,1)}), bf16[16,64,512]{2,1,0:T(8,128)(2,1)S(1)}, u32[]{:S(2)}, u32[]{:S(2)}) async-start(bf16[16,64,512]{2,1,0:T(8,128)(2,1)} %fusion.25), calls=%async_computation | async-start | bytes 2097152 | tf_op jit(solution)/shard_map/all_to_all | solution.py:79
  10.2 16.1 %all-to-all-done = bf16[16,64,512]{2,1,0:T(8,128)(2,1)S(1)} async-done(((bf16[16,64,512]{2,1,0:T(8,128)(2,1)}), bf16[16,64,512]{2,1,0:T(8,128)(2,1)S(1)}, u32[]{:S(2)}, u32[]{:S(2)}) %all-to-all-start) | async-done | bytes 1048608 | tf_op jit(solution)/shard_map/all_to_all | solution.py:79
  26.3 2.6 %collective-permute-start.2 = (bf16[16,64,512]{2,1,0:T(8,128)(2,1)S(1)}, bf16[16,64,512]{2,1,0:T(8,128)(2,1)S(1)}, u32[]{:S(2)}, u32[]{:S(2)}) collective-permute-start(bf16[16,64,512]{2,1,0:T(8,128)(2,1)S(1)} %all-to-all-done), channel_id=1, source_target_pairs={{0,16},{1,17},{2,18},{3,19},{4,20},{5,21},{6,22},{7,23},{8,24},{9,... | collective-permute-start | bytes 3145736 | tf_op jit(solution)/shard_map/ppermute | solution.py:96
  28.9 5.5 %fusion.3 = f32[64,1,256]{2,1,0:T(1,128)S(1)} fusion(f32[64,128,1]{1,2,0:T(1,128)S(1)} %bitcast.62, bf16[256,8192]{1,0:T(8,128)(2,1)} %param.10), kind=kOutput, calls=%fused_computation.5 | convolution fusion | flops 25165824 | bytes 4292608 | tf_op jit(solution)/shard_map/dhj,hj->hd/dot_general | solution.py:109
  34.5 0.7 collective-permute-start
  35.1 3.3 %collective-permute-start.1 = (f32[32,256]{1,0:T(8,128)S(1)}, f32[32,256]{1,0:T(8,128)S(1)}, u32[]{:S(2)}, u32[]{:S(2)}) collective-permute-start(f32[32,256]{1,0:T(8,128)S(1)} %get-tuple-element.13), channel_id=1, source_target_pairs={{0,16},{1,0},{2,17},{3,1},{4,18},{5,2},{6,19},{7,3},{8,20},{9,4},{... | collective-permute-start | bytes 98312 | tf_op jit(solution)/shard_map/ppermute | solution.py:120
  38.5 13.3 %collective-permute-done.1 = f32[32,256]{1,0:T(8,128)S(1)} collective-permute-done((f32[32,256]{1,0:T(8,128)S(1)}, f32[32,256]{1,0:T(8,128)S(1)}, u32[]{:S(2)}, u32[]{:S(2)}) %collective-permute-start.1) | collective-permute-done | bytes 32800 | tf_op jit(solution)/shard_map/ppermute | solution.py:120
  51.8 23.3 %collective-permute-done.2 = bf16[16,64,512]{2,1,0:T(8,128)(2,1)S(1)} collective-permute-done((bf16[16,64,512]{2,1,0:T(8,128)(2,1)S(1)}, bf16[16,64,512]{2,1,0:T(8,128)(2,1)S(1)}, u32[]{:S(2)}, u32[]{:S(2)}) %collective-permute-start.2) | collective-permute-done | bytes 1048608 | tf_op jit(solution)/shard_map/ppermute | solution.py:96
  75.6 0.3 reshape.100
  75.9 1.8 add_convert_fusion
  77.7 2.6 %copy-done.1 = bf16[96,64,512]{2,1,0:T(8,128)(2,1)} copy-done((bf16[96,64,512]{2,1,0:T(8,128)(2,1)}, bf16[96,64,512]{2,1,0:T(8,128)(2,1)S(1)}, u32[]{:S(2)}) %copy-start.1) | copy-done | bytes 6291480
  80.3 2.0 convolution_reduce_fusion
  82.3 1.0 reshape.103
  83.4 3.8 %all-to-all-start.1 = ((f32[16,96,128]{2,1,0:T(8,128)}), f32[16,96,128]{2,1,0:T(8,128)S(1)}, u32[]{:S(2)}, u32[]{:S(2)}) async-start(f32[16,96,128]{2,1,0:T(8,128)} %reshape.103), calls=%async_computation.1 | async-start | bytes 1572864 | tf_op jit(solution)/shard_map/all_to_all | solution.py:79
  87.3 13.1 %all-to-all-done.1 = f32[16,96,128]{2,1,0:T(8,128)S(1)} async-done(((f32[16,96,128]{2,1,0:T(8,128)}), f32[16,96,128]{2,1,0:T(8,128)S(1)}, u32[]{:S(2)}, u32[]{:S(2)}) %all-to-all-start.1) | async-done | bytes 786464 | tf_op jit(solution)/shard_map/all_to_all | solution.py:79
  101.1 11.7 %all_to_all.25 = bf16[16,96,128]{2,1,0:T(8,128)(2,1)S(1)} all-to-all(bf16[16,96,128]{2,1,0:T(8,128)(2,1)S(1)} %broadcast_in_dim.25), channel_id=1, replica_groups={{0,1,2,3,4,5,6,7,8,9,10,11,12,13,14,15},{16,17,18,19,20,21,22,23,24,25,..., dimensions={0} | all-to-all | bytes 786432 | tf_op jit(solution)/shard_map/all_to_all | solution.py:79
  112.8 0.3 reshape.104
  113.2 0.8 copy.22
  114.0 9.5 %fusion.11 = bf16[64,32,512]{2,1,0:T(8,128)(2,1)S(1)} fusion(bf16[32,96,64]{1,0,2:T(8,128)(2,1)S(1)} %copy.22, bf16[96,64,512]{2,1,0:T(8,128)(2,1)} %copy-done.1), kind=kOutput, calls=%fused_computation.16 | convolution fusion | flops 202375168 | bytes 8781824 | tf_op jit(solution)/shard_map/hvt,vtd->thd/dot_general | solution.py:144
  123.6 2.5 %copy.30 = bf16[64,32,512]{2,0,1:T(8,128)(2,1)} copy(bf16[64,32,512]{2,1,0:T(8,128)(2,1)S(1)} %fusion.11) | data formatting | bytes 4194304 | tf_op jit(solution)/shard_map/reshape | solution.py:147
  126.0 3.9 %all-to-all-start.3 = ((bf16[16,128,512]{2,1,0:T(8,128)(2,1)}), bf16[16,128,512]{2,1,0:T(8,128)(2,1)S(1)}, u32[]{:S(2)}, u32[]{:S(2)}) async-start(bf16[16,128,512]{2,1,0:T(8,128)(2,1)} %bitcast.15), calls=%async_computation.3 | async-start | bytes 4194304 | tf_op jit(solution)/shard_map/all_to_all | solution.py:79
  130.0 6.0 %copy.34 = bf16[32,8,16,512]{3,2,1,0:T(8,128)(2,1)} copy(bf16[32,8,16,512]{3,1,2,0:T(8,128)(2,1)} %bitcast.65) | data formatting | bytes 8388608
  136.0 22.8 %all-to-all-done.3 = bf16[16,128,512]{2,1,0:T(8,128)(2,1)S(1)} async-done(((bf16[16,128,512]{2,1,0:T(8,128)(2,1)}), bf16[16,128,512]{2,1,0:T(8,128)(2,1)S(1)}, u32[]{:S(2)}, u32[]{:S(2)}) %all-to-all-start.3) | async-done | bytes 2097184 | tf_op jit(solution)/shard_map/all_to_all | solution.py:79
  158.8 6.9 %fusion.21 = bf16[2,8,8,128]{3,2,1,0:T(8,128)(2,1)S(1)} fusion(bf16[16,2,64,512]{3,2,1,0:T(8,128)(2,1)S(1)} %bitcast.69, bf16[2,128,16,512]{3,2,1,0:T(8,128)(2,1)} %bitcast.66), kind=kOutput, calls=%fused_computation.21 | convolution fusion | flops 268451840 | bytes 6324224 | tf_op jit(solution)/shard_map/rhtk,hcrk->thc/dot_general | solution.py:151
  165.8 0.8 convolution_convert_fusion
  166.6 0.5 reshape.109
  167.2 31.2 %all_to_all.26 = bf16[32,16,1024]{2,1,0:T(8,128)(2,1)S(1)} all-to-all(bf16[32,16,1024]{2,1,0:T(8,128)(2,1)S(1)} %reshape.109), channel_id=1, replica_groups=mesh['dev'=32] {'dev'}, dimensions={0} | all-to-all | bytes 2097152 | tf_op jit(solution)/shard_map/all_to_all | solution.py:159
  198.5 0.6 convert_element_type.64
  (34 shorter events, 1.6 us)
Async XLA Ops:
  0.0 28.9 %copy-start = (f32[8192]{0:T(1024)S(1)}, f32[8192]{0:T(1024)}, u32[]{:S(2)}) copy-start(f32[8192]{0:T(1024)} %param.11) | copy-start | bytes 98308
  0.0 2.7 %copy-start.3 = (bf16[3,8192]{1,0:T(4,128)(2,1)S(1)}, bf16[3,8192]{1,0:T(4,128)(2,1)}, u32[]{:S(2)}) copy-start(bf16[3,8192]{1,0:T(4,128)(2,1)} %param.9) | copy-start | bytes 147460
  3.8 22.5 %all-to-all-start = ((bf16[16,64,512]{2,1,0:T(8,128)(2,1)}), bf16[16,64,512]{2,1,0:T(8,128)(2,1)S(1)}, u32[]{:S(2)}, u32[]{:S(2)}) async-start(bf16[16,64,512]{2,1,0:T(8,128)(2,1)} %fusion.25), calls=%async_computation | async-start | bytes 2097152 | tf_op jit(solution)/shard_map/all_to_all | solution.py:79
  26.3 48.8 %collective-permute-start.2 = (bf16[16,64,512]{2,1,0:T(8,128)(2,1)S(1)}, bf16[16,64,512]{2,1,0:T(8,128)(2,1)S(1)}, u32[]{:S(2)}, u32[]{:S(2)}) collective-permute-start(bf16[16,64,512]{2,1,0:T(8,128)(2,1)S(1)} %all-to-all-done), channel_id=1, source_target_pairs={{0,16},{1,17},{2,18},{3,19},{4,20},{5,21},{6,22},{7,23},{8,24},{9,... | collective-permute-start | bytes 3145736 | tf_op jit(solution)/shard_map/ppermute | solution.py:96
  34.5 4.0 %collective-permute-start = (f32[32,256]{1,0:T(8,128)S(1)}, f32[32,256]{1,0:T(8,128)S(1)}, u32[]{:S(2)}, u32[]{:S(2)}) collective-permute-start(f32[32,256]{1,0:T(8,128)S(1)} %get-tuple-element.12), channel_id=1, source_target_pairs={{0,0},{1,16},{2,1},{3,17},{4,2},{5,18},{6,3},{7,19},{8,4},{9,20},{... | collective-permute-start | bytes 98312 | tf_op jit(solution)/shard_map/ppermute | solution.py:119
  35.1 16.6 %collective-permute-start.1 = (f32[32,256]{1,0:T(8,128)S(1)}, f32[32,256]{1,0:T(8,128)S(1)}, u32[]{:S(2)}, u32[]{:S(2)}) collective-permute-start(f32[32,256]{1,0:T(8,128)S(1)} %get-tuple-element.13), channel_id=1, source_target_pairs={{0,16},{1,0},{2,17},{3,1},{4,18},{5,2},{6,19},{7,3},{8,20},{9,4},{... | collective-permute-start | bytes 98312 | tf_op jit(solution)/shard_map/ppermute | solution.py:120
  77.7 2.6 %copy-start.1 = (bf16[96,64,512]{2,1,0:T(8,128)(2,1)}, bf16[96,64,512]{2,1,0:T(8,128)(2,1)S(1)}, u32[]{:S(2)}) copy-start(bf16[96,64,512]{2,1,0:T(8,128)(2,1)S(1)} %add_convert_fusion) | copy-start | bytes 18874372
  83.4 17.1 %all-to-all-start.1 = ((f32[16,96,128]{2,1,0:T(8,128)}), f32[16,96,128]{2,1,0:T(8,128)S(1)}, u32[]{:S(2)}, u32[]{:S(2)}) async-start(f32[16,96,128]{2,1,0:T(8,128)} %reshape.103), calls=%async_computation.1 | async-start | bytes 1572864 | tf_op jit(solution)/shard_map/all_to_all | solution.py:79
  126.0 32.8 %all-to-all-start.3 = ((bf16[16,128,512]{2,1,0:T(8,128)(2,1)}), bf16[16,128,512]{2,1,0:T(8,128)(2,1)S(1)}, u32[]{:S(2)}, u32[]{:S(2)}) async-start(bf16[16,128,512]{2,1,0:T(8,128)(2,1)} %bitcast.15), calls=%async_computation.3 | async-start | bytes 4194304 | tf_op jit(solution)/shard_map/all_to_all | solution.py:79
  158.8 6.9 %copy-start.2 = (bf16[256,8192]{1,0:T(8,128)(2,1)S(1)}, bf16[256,8192]{1,0:T(8,128)(2,1)}, u32[]{:S(2)}) copy-start(bf16[256,8192]{1,0:T(8,128)(2,1)} %param.13) | copy-start | bytes 12582916

commit v2 on v1

--- a/solution.py
+++ b/solution.py
@@ -2,6 +2,7 @@
 import jax.numpy as jnp
 from jax import lax
 from jax.sharding import PartitionSpec as P
+
 
 D = 8192
 HEADS = 64
@@ -67,7 +68,11 @@
     return [piece.astype(jnp.bfloat16) for piece in (hi, mid, low)]
 
 
-def halves_body(pixels, embed_w, var_embed, key_w, query, value_t, out_w):
+def halves_body(*args):
+    return halves_plan(*args)
+
+
+def halves_plan(pixels, embed_w, var_embed, key_w, query, value_t, out_w):
     n_dev = lax.axis_size("dev")
     half = n_dev // 2
     me = lax.axis_index("dev")
@@ -84,24 +89,42 @@
     half_heads = HEADS // 2
     dev_heads = HEADS // n_dev
 
-    w_rows = embed_w.reshape(own_v, p_size, half, width).transpose(2, 0, 1, 3)
-    w_rows = w_rows.reshape(half, own_v * p_size, width)
-    var_rows = var_embed.reshape(own_v, half, width).transpose(1, 0, 2)
-    pix_rows = pixels.transpose(0, 2, 1).reshape(1, -1, width)
+    first = my_half == 0
+    cut = p_size // 2
+
+    def by_slice(x):
+        x = x.reshape(x.shape[0], -1, half, width).transpose(2, 0, 1, 3)
+        return x.reshape(half, -1, width)
+
+    def in_order(mine, other):
+        return [jnp.where(first, mine, other), jnp.where(first, other, mine)]
+
+    pix_lanes = pixels.transpose(0, 2, 1).reshape(own_v, p_size * tokens)
+    small = jnp.concatenate([var_embed, pix_lanes], axis=1)
+    small_other = lax.ppermute(small, "dev", across)
+    early = embed_w[:, :cut]
+    early_other = lax.ppermute(early, "dev", across)
+    small_both = jnp.concatenate(in_order(small, small_other), axis=0)
+    var_rows = by_slice(small_both[:, :D])
+    pix_rows = small_both[:, D:].reshape(1, -1, width)
     pix_rows = jnp.broadcast_to(pix_rows, (half,) + pix_rows.shape[1:])
-    packed = jnp.concatenate([w_rows, var_rows, pix_rows], axis=1)
+    packed = jnp.concatenate([by_slice(embed_w[:, cut:]), var_rows, pix_rows], axis=1)
     n_rows = packed.shape[1]
     packed = jnp.pad(packed, ((0, 0), (0, -n_rows % 16), (0, 0)))
-    mine = exchange(packed)
-    other = lax.ppermute(mine, "dev", across)
-    first = my_half == 0
-    both = jnp.concatenate(
-        [jnp.where(first, mine, other), jnp.where(first, other, mine)], axis=0
-    )
-    k = own_v * p_size
-    w_all = both[:, :k].reshape(slots, p_size, width)
-    var_all = both[:, k : k + own_v].reshape(slots, width)
-    pix_all = both[:, k + own_v : n_rows].reshape(slots, p_size, tokens)
+    packed = exchange(packed)
+    k = own_v * (p_size - cut)
+    late = packed[:, :k]
+    late_other = lax.ppermute(late, "dev", across)
+    early_other, late = lax.optimization_barrier((early_other, late))
+    small_v = packed[:, k : k + 2 * own_v].reshape(half, 2, own_v, width)
+    var_all = small_v.transpose(1, 0, 2, 3).reshape(slots, width)
+    pix_all = packed[:, k + 2 * own_v : n_rows].reshape(half, 2, own_v, p_size, tokens)
+    pix_all = pix_all.transpose(1, 0, 2, 3, 4).reshape(slots, p_size, tokens)
+    early = by_slice(jnp.concatenate(in_order(early, early_other), axis=0))
+    early = exchange(early)
+    early = early.reshape(half, 2, own_v, cut, width).transpose(1, 0, 2, 3, 4)
+    late = jnp.stack(in_order(late, late_other)).reshape(2, half, own_v, -1, width)
+    w_all = jnp.concatenate([early, late], axis=3).reshape(slots, p_size, width)
     embed = jnp.einsum("vpt,vpd->vtd", pix_all, w_all, preferred_element_type=jnp.float32)
     embed = (embed + var_all.astype(jnp.float32)[:, None, :]).astype(jnp.bfloat16)
 
@@ -155,9 +178,20 @@
         preferred_element_type=jnp.float32,
     )
     value_heads = value_heads.reshape(tokens, columns).astype(jnp.bfloat16)
-    sums = jnp.dot(value_heads, out_w, preferred_element_type=jnp.float32).astype(jnp.bfloat16)
+    side = me % 2
+    rows = value_heads.reshape(half, 2, -1, columns).transpose(1, 0, 2, 3)
+    rows = rows.reshape(2, tokens // 2, columns)
+
+    def sums_for(who):
+        picked = lax.dynamic_index_in_dim(rows, who, 0, keepdims=False)
+        return jnp.dot(picked, out_w, preferred_element_type=jnp.float32)
+
+    swap = [(i, i ^ 1) for i in range(n_dev)]
+    sums = lax.ppermute(sums_for(1 - side), "dev", swap) + sums_for(side)
+    same_side = [[2 * i + c for i in range(half)] for c in range(2)]
     sums = lax.all_to_all(
-        sums.reshape(n_dev, -1, 1024), "dev", 0, 0, tiled=True
+        sums.astype(jnp.bfloat16).reshape(half, -1, 1024),
+        "dev", 0, 0, axis_index_groups=same_side, tiled=True,
     )
     summed = jnp.sum(sums.astype(jnp.float32), axis=0)
     return summed.reshape(tokens // n_dev, D).astype(jnp.bfloat16)
@@ -174,7 +208,8 @@
         P("dev", None),
     )
     n_dev = mesh.shape["dev"]
-    chosen = halves_body if n_dev % 2 == 0 and HEADS % n_dev == 0 else body
+    halves = n_dev % 2 == 0 and HEADS % n_dev == 0
+    chosen = halves_body if halves else body
     return jax.shard_map(
         chosen, mesh=mesh, in_specs=placed, out_specs=P("dev", None), check_vma=False
     )

time: 200 us -> 198 us (0.990)
  starting transfers between devices: 20.6 us -> 33.1 us
  waiting for transfers between devices: 88.7 us -> 77.9 us
  blocking collectives: 43 us -> 33.7 us
  matrix products: 26.7 us -> 29.6 us
  local copies, waits for them, and re-layouts: 18 us -> 20.6 us
    ppermute x3 -> x6, waiting for transfers between devices: 36.6 us -> 23.5 us  [the longest x1 16.9 us: halves_plan(): late_other = lax.ppermute(late, 'dev', across)]
    ppermute x3 -> x6, starting transfers between devices: 6.58 us -> 16.1 us  [the longest x1 4.69 us: halves_plan(): lax.ppermute(jnp.where(odd == 0, high_heads, low_heads), 'dev', to_other)]
    all_to_all x1, blocking collectives: 31.2 us -> 22 us  [halves_plan(): lax.all_to_all(sums.astype(jnp.bfloat16).reshape(half, -1, 1024), 'dev',...]
    dot_general x6 -> x7, matrix products: 26.7 us -> 29.6 us  [the longest x1 9.54 us: halves_plan(): jnp.einsum('hvt,vtd->thd', attn, embed, preferred_element_type=jnp.float32)]
    all_to_all x3 -> x4, starting transfers between devices: 14 us -> 17 us  [exchange(): return lax.all_to_all(x, 'dev', 0, 0, axis_index_groups=in_half, tiled=True)]
    all_to_all x3 -> x4, waiting for transfers between devices: 52.1 us -> 54.4 us  [exchange(): return lax.all_to_all(x, 'dev', 0, 0, axis_index_groups=in_half, tiled=True)]
    reshape x6 -> x7, local copies, waits for them, and re-layouts: 5.47 us -> 6 us  [the longest x1 2.49 us: halves_plan(): pooled.reshape(tokens, half, dev_heads, width).transpose(1, 2, 0, 3)]
    unnamed x10 -> x13, local copies, waits for them, and re-layouts: 10 us -> 10 us
  transfers between devices with their start and end apart: 6 -> 10, of which waited for: 5 -> 7; matrix products, arithmetic and copies ran while one was open for 6% -> 7% of each run, Pallas kernels for 0% -> 0%
where the time goes in v2:
time: 198 us; the launch traced here: 197 us
  waiting for transfers between devices  77.9 us (39%)
  blocking collectives  33.7 us (17%)
  starting transfers between devices  33.1 us (17%)
  matrix products  29.6 us (15%)
  local copies, waits for them, and re-layouts  20.6 us (10%)
  other arithmetic  2.01 us (1%)
    all_to_all x4, waiting for transfers between devices, exchange(): return lax.all_to_all(x, 'dev', 0, 0, axis_index_groups=in_half, tiled=True)  54.4 us
    all_to_all x1, blocking collectives, halves_plan(): lax.all_to_all(sums.astype(jnp.bfloat16).reshape(half, -1, 1024), 'dev',...  22 us
    all_to_all x4, starting transfers between devices, exchange(): return lax.all_to_all(x, 'dev', 0, 0, axis_index_groups=in_half, tiled=True)  17 us
    ppermute x1, waiting for transfers between devices, halves_plan(): late_other = lax.ppermute(late, 'dev', across)  16.9 us
    all_to_all x1, blocking collectives, exchange(): return lax.all_to_all(x, 'dev', 0, 0, axis_index_groups=in_half, tiled=True)  11.7 us
    unnamed x13, local copies, waits for them, and re-layouts  10 us
    dot_general x1, matrix products, halves_plan(): jnp.einsum('hvt,vtd->thd', attn, embed, preferred_element_type=jnp.float32)  9.54 us
    dot_general x1, matrix products, halves_plan(): jnp.einsum('rhtk,hcrk->thc', received, value_t.reshape(dev_heads, columns...  6.77 us
  transfers between devices with their start and end apart: 10, of which 7 were waited for; matrix products, arithmetic and copies ran while one was open for 7% of the time, Pallas kernels for 0%

profile of v2, /device:TPU:0, one launch (start us, length us, event | category | flops | bytes accessed | tf_op | source)
XLA Modules:
  0.0 197.4 jit_solution(3941362139146184900)
XLA Ops:
  0.0 0.9 constant_dynamic-update-slice_fusion.1
  1.8 4.1 %collective-permute-start.2 = (bf16[3,9216]{1,0:T(4,128)(2,1)S(1)}, bf16[3,9216]{1,0:T(4,128)(2,1)S(1)}, u32[]{:S(2)}, u32[]{:S(2)}) collective-permute-start(bf16[3,9216]{1,0:T(4,128)(2,1)S(1)} %constant_dynamic-update-slice_fusion), channel_id=1, source_target_pairs={{0,16},{1,17},{2,18},{3,19},{4,20},{5,21},{6,22},{7,23},{8,24},{9,... | collective-permute-start | bytes 165896 | tf_op jit(solution)/shard_map/ppermute | solution.py:104
  5.9 1.2 fusion.41
  7.4 2.4 %collective-permute-done.2 = bf16[3,9216]{1,0:T(4,128)(2,1)S(1)} collective-permute-done((bf16[3,9216]{1,0:T(4,128)(2,1)S(1)}, bf16[3,9216]{1,0:T(4,128)(2,1)S(1)}, u32[]{:S(2)}, u32[]{:S(2)}) %collective-permute-start.2) | collective-permute-done | bytes 55328 | tf_op jit(solution)/shard_map/ppermute | solution.py:104
  10.0 1.0 fusion.25
  11.0 4.0 %all-to-all-start = ((bf16[16,48,512]{2,1,0:T(8,128)(2,1)}), bf16[16,48,512]{2,1,0:T(8,128)(2,1)S(1)}, u32[]{:S(2)}, u32[]{:S(2)}) async-start(bf16[16,48,512]{2,1,0:T(8,128)(2,1)} %fusion.25), calls=%async_computation | async-start | bytes 1572864 | tf_op jit(solution)/shard_map/all_to_all | solution.py:84
  15.1 3.3 %collective-permute-start.3 = (bf16[3,8,8192]{2,1,0:T(8,128)(2,1)S(1)}, bf16[3,8,8192]{2,1,0:T(8,128)(2,1)S(1)}, u32[]{:S(2)}, u32[]{:S(2)}) collective-permute-start(bf16[3,8,8192]{2,1,0:T(8,128)(2,1)S(1)} %get-tuple-element.13), channel_id=1, source_target_pairs={{0,16},{1,17},{2,18},{3,19},{4,20},{5,21},{6,22},{7,23},{8,24},{9,... | collective-permute-start | bytes 1179656 | tf_op jit(solution)/shard_map/ppermute | solution.py:106
  18.4 18.4 %all-to-all-done = bf16[16,48,512]{2,1,0:T(8,128)(2,1)S(1)} async-done(((bf16[16,48,512]{2,1,0:T(8,128)(2,1)}), bf16[16,48,512]{2,1,0:T(8,128)(2,1)S(1)}, u32[]{:S(2)}, u32[]{:S(2)}) %all-to-all-start) | async-done | bytes 786464 | tf_op jit(solution)/shard_map/all_to_all | solution.py:84
  37.3 1.3 copy.121
  38.6 4.6 %all-to-all-start.1 = ((bf16[16,48,512]{2,1,0:T(8,128)(2,1)}), bf16[16,48,512]{2,1,0:T(8,128)(2,1)S(1)}, u32[]{:S(2)}, u32[]{:S(2)}) async-start(bf16[16,48,512]{2,1,0:T(8,128)(2,1)} %bitcast.92), calls=%async_computation.1 | async-start | bytes 1572864 | tf_op jit(solution)/shard_map/all_to_all | solution.py:84
  43.2 5.5 %fusion.4 = f32[64,1,256]{2,1,0:T(1,128)S(1)} fusion(f32[64,128,1]{1,2,0:T(1,128)S(1)} %bitcast.97, bf16[256,8192]{1,0:T(8,128)(2,1)} %param.10), kind=kOutput, calls=%fused_computation.6 | convolution fusion | flops 25165824 | bytes 4292608 | tf_op jit(solution)/shard_map/dhj,hj->hd/dot_general | solution.py:132
  49.5 4.7 %collective-permute-start.1 = (f32[32,256]{1,0:T(8,128)S(1)}, f32[32,256]{1,0:T(8,128)S(1)}, u32[]{:S(2)}, u32[]{:S(2)}) collective-permute-start(f32[32,256]{1,0:T(8,128)S(1)} %get-tuple-element.23), channel_id=1, source_target_pairs={{0,16},{1,0},{2,17},{3,1},{4,18},{5,2},{6,19},{7,3},{8,20},{9,4},{... | collective-permute-start | bytes 98312 | tf_op jit(solution)/shard_map/ppermute | solution.py:143
  54.2 1.6 collective-permute-done.1
  55.8 3.3 %collective-permute-start.4 = (bf16[16,24,512]{2,1,0:T(8,128)(2,1)S(1)}, bf16[16,24,512]{2,1,0:T(8,128)(2,1)S(1)}, u32[]{:S(2)}, u32[]{:S(2)}) collective-permute-start(bf16[16,24,512]{2,1,0:T(8,128)(2,1)S(1)} %slice.41), channel_id=1, source_target_pairs={{0,16},{1,17},{2,18},{3,19},{4,20},{5,21},{6,22},{7,23},{8,24},{9,... | collective-permute-start | bytes 1179656 | tf_op jit(solution)/shard_map/ppermute | solution.py:117
  59.8 16.9 %collective-permute-done.4 = bf16[16,24,512]{2,1,0:T(8,128)(2,1)S(1)} collective-permute-done((bf16[16,24,512]{2,1,0:T(8,128)(2,1)S(1)}, bf16[16,24,512]{2,1,0:T(8,128)(2,1)S(1)}, u32[]{:S(2)}, u32[]{:S(2)}) %collective-permute-start.4) | collective-permute-done | bytes 393248 | tf_op jit(solution)/shard_map/ppermute | solution.py:117
  77.1 1.8 add_convert_fusion
  78.9 2.6 %copy-done.1 = bf16[96,64,512]{2,1,0:T(8,128)(2,1)} copy-done((bf16[96,64,512]{2,1,0:T(8,128)(2,1)}, bf16[96,64,512]{2,1,0:T(8,128)(2,1)S(1)}, u32[]{:S(2)}) %copy-start.1) | copy-done | bytes 6291480
  81.6 2.0 %convolution_reduce_fusion = f32[32,6144]{1,0:T(8,128)S(1)} fusion(bf16[3,32,512]{2,1,0:T(8,128)(2,1)S(1)} %bitcast.112, bf16[6144,512,1]{1,0,2:T(8,128)(2,1)S(1)} %bitcast.98), kind=kOutput, calls=%fused_computation.17 | convolution fusion | flops 604372992 | bytes 7176192 | tf_op jit(solution)/shard_map/dot_general | solution.py:148
  83.5 1.1 reshape.140
  84.6 4.4 %all-to-all-start.2 = ((f32[16,96,128]{2,1,0:T(8,128)}), f32[16,96,128]{2,1,0:T(8,128)S(1)}, u32[]{:S(2)}, u32[]{:S(2)}) async-start(f32[16,96,128]{2,1,0:T(8,128)} %reshape.140), calls=%async_computation.2 | async-start | bytes 1572864 | tf_op jit(solution)/shard_map/all_to_all | solution.py:84
  89.2 13.1 %all-to-all-done.2 = f32[16,96,128]{2,1,0:T(8,128)S(1)} async-done(((f32[16,96,128]{2,1,0:T(8,128)}), f32[16,96,128]{2,1,0:T(8,128)S(1)}, u32[]{:S(2)}, u32[]{:S(2)}) %all-to-all-start.2) | async-done | bytes 786464 | tf_op jit(solution)/shard_map/all_to_all | solution.py:84
  103.0 11.7 %all_to_all.30 = bf16[16,96,128]{2,1,0:T(8,128)(2,1)S(1)} all-to-all(bf16[16,96,128]{2,1,0:T(8,128)(2,1)S(1)} %broadcast_in_dim.25), channel_id=1, replica_groups={{0,1,2,3,4,5,6,7,8,9,10,11,12,13,14,15},{16,17,18,19,20,21,22,23,24,25,..., dimensions={0} | all-to-all | bytes 786432 | tf_op jit(solution)/shard_map/all_to_all | solution.py:84
  115.0 0.8 copy.74
  115.9 9.5 %fusion.9 = bf16[64,32,512]{2,1,0:T(8,128)(2,1)S(1)} fusion(bf16[32,96,64]{1,0,2:T(8,128)(2,1)S(1)} %copy.74, bf16[96,64,512]{2,1,0:T(8,128)(2,1)} %copy-done.1), kind=kOutput, calls=%fused_computation.11 | convolution fusion | flops 202375168 | bytes 8781824 | tf_op jit(solution)/shard_map/hvt,vtd->thd/dot_general | solution.py:167
  125.4 2.5 %copy.83 = bf16[64,32,512]{2,0,1:T(8,128)(2,1)} copy(bf16[64,32,512]{2,1,0:T(8,128)(2,1)S(1)} %fusion.9) | data formatting | bytes 4194304 | tf_op jit(solution)/shard_map/reshape | solution.py:170
  127.9 3.9 %all-to-all-start.4 = ((bf16[16,128,512]{2,1,0:T(8,128)(2,1)}), bf16[16,128,512]{2,1,0:T(8,128)(2,1)S(1)}, u32[]{:S(2)}, u32[]{:S(2)}) async-start(bf16[16,128,512]{2,1,0:T(8,128)(2,1)} %bitcast.26), calls=%async_computation.4 | async-start | bytes 4194304 | tf_op jit(solution)/shard_map/all_to_all | solution.py:84
  131.9 6.0 %copy.90 = bf16[32,8,16,512]{3,2,1,0:T(8,128)(2,1)} copy(bf16[32,8,16,512]{3,1,2,0:T(8,128)(2,1)} %bitcast.100) | data formatting | bytes 8388608
  137.9 22.8 %all-to-all-done.4 = bf16[16,128,512]{2,1,0:T(8,128)(2,1)S(1)} async-done(((bf16[16,128,512]{2,1,0:T(8,128)(2,1)}), bf16[16,128,512]{2,1,0:T(8,128)(2,1)S(1)}, u32[]{:S(2)}, u32[]{:S(2)}) %all-to-all-start.4) | async-done | bytes 2097184 | tf_op jit(solution)/shard_map/all_to_all | solution.py:84
  160.7 6.8 %fusion.21 = bf16[64,2,128]{2,0,1:T(8,128)(2,1)S(1)} fusion(bf16[16,2,64,512]{3,2,1,0:T(8,128)(2,1)S(1)} %bitcast.105, bf16[2,128,16,512]{3,2,1,0:T(8,128)(2,1)} %bitcast.101), kind=kOutput, calls=%fused_computation.20 | convolution fusion | flops 268451840 | bytes 6324224 | tf_op jit(solution)/shard_map/rhtk,hcrk->thc/dot_general | solution.py:174
  167.7 3.2 %fusion.37 = f32[32,8192]{1,0:T(8,128)S(1)} fusion(bf16[256,8192]{1,0:T(8,128)(2,1)} %param.13, bf16[1,32,256]{2,0,1:T(2,128)(2,1)S(1)} %get-tuple-element.25), kind=kOutput, calls=%fused_computation.62 | convolution fusion | flops 134217728 | bytes 5259264 | tf_op jit(solution)/shard_map/dot_general | solution.py:187
  170.9 2.6 %collective-permute-done.5 = f32[32,8192]{1,0:T(8,128)S(1)} collective-permute-done((f32[32,8192]{1,0:T(8,128)S(1)}, f32[32,8192]{1,0:T(8,128)S(1)}, u32[]{:S(2)}, u32[]{:S(2)}) %collective-permute-start.5) | collective-permute-done | bytes 1048608 | tf_op jit(solution)/shard_map/ppermute | solution.py:190
  174.6 22.0 %all_to_all.31 = bf16[16,16,1024]{2,1,0:T(8,128)(2,1)S(1)} all-to-all(bf16[16,16,1024]{2,1,0:T(8,128)(2,1)S(1)} %reshape.147), channel_id=1, replica_groups={{0,2,4,6,8,10,12,14,16,18,20,22,24,26,28,30},{1,3,5,7,9,11,13,15,17,19,..., dimensions={0} | all-to-all | bytes 1048576 | tf_op jit(solution)/shard_map/all_to_all | solution.py:192
  (63 shorter events, 6.6 us)
Async XLA Ops:
  0.0 43.2 %copy-start = (f32[8192]{0:T(1024)S(1)}, f32[8192]{0:T(1024)}, u32[]{:S(2)}) copy-start(f32[8192]{0:T(1024)} %param.11) | copy-start | bytes 98308
  0.0 36.9 %copy-start.3 = (bf16[3,16,8192]{2,1,0:T(8,128)(2,1)S(1)}, bf16[3,16,8192]{2,1,0:T(8,128)(2,1)}, u32[]{:S(2)}) copy-start(bf16[3,16,8192]{2,1,0:T(8,128)(2,1)} %param.8) | copy-start | bytes 2359300
  1.8 8.0 %collective-permute-start.2 = (bf16[3,9216]{1,0:T(4,128)(2,1)S(1)}, bf16[3,9216]{1,0:T(4,128)(2,1)S(1)}, u32[]{:S(2)}, u32[]{:S(2)}) collective-permute-start(bf16[3,9216]{1,0:T(4,128)(2,1)S(1)} %constant_dynamic-update-slice_fusion), channel_id=1, source_target_pairs={{0,16},{1,17},{2,18},{3,19},{4,20},{5,21},{6,22},{7,23},{8,24},{9,... | collective-permute-start | bytes 165896 | tf_op jit(solution)/shard_map/ppermute | solution.py:104
  11.0 25.8 %all-to-all-start = ((bf16[16,48,512]{2,1,0:T(8,128)(2,1)}), bf16[16,48,512]{2,1,0:T(8,128)(2,1)S(1)}, u32[]{:S(2)}, u32[]{:S(2)}) async-start(bf16[16,48,512]{2,1,0:T(8,128)(2,1)} %fusion.25), calls=%async_computation | async-start | bytes 1572864 | tf_op jit(solution)/shard_map/all_to_all | solution.py:84
  15.1 21.8 %collective-permute-start.3 = (bf16[3,8,8192]{2,1,0:T(8,128)(2,1)S(1)}, bf16[3,8,8192]{2,1,0:T(8,128)(2,1)S(1)}, u32[]{:S(2)}, u32[]{:S(2)}) collective-permute-start(bf16[3,8,8192]{2,1,0:T(8,128)(2,1)S(1)} %get-tuple-element.13), channel_id=1, source_target_pairs={{0,16},{1,17},{2,18},{3,19},{4,20},{5,21},{6,22},{7,23},{8,24},{9,... | collective-permute-start | bytes 1179656 | tf_op jit(solution)/shard_map/ppermute | solution.py:106
  38.6 38.1 %all-to-all-start.1 = ((bf16[16,48,512]{2,1,0:T(8,128)(2,1)}), bf16[16,48,512]{2,1,0:T(8,128)(2,1)S(1)}, u32[]{:S(2)}, u32[]{:S(2)}) async-start(bf16[16,48,512]{2,1,0:T(8,128)(2,1)} %bitcast.92), calls=%async_computation.1 | async-start | bytes 1572864 | tf_op jit(solution)/shard_map/all_to_all | solution.py:84
  48.8 5.4 %collective-permute-start = (f32[32,256]{1,0:T(8,128)S(1)}, f32[32,256]{1,0:T(8,128)S(1)}, u32[]{:S(2)}, u32[]{:S(2)}) collective-permute-start(f32[32,256]{1,0:T(8,128)S(1)} %get-tuple-element.22), channel_id=1, source_target_pairs={{0,0},{1,16},{2,1},{3,17},{4,2},{5,18},{6,3},{7,19},{8,4},{9,20},{... | collective-permute-start | bytes 98312 | tf_op jit(solution)/shard_map/ppermute | solution.py:142
  49.5 6.3 %collective-permute-start.1 = (f32[32,256]{1,0:T(8,128)S(1)}, f32[32,256]{1,0:T(8,128)S(1)}, u32[]{:S(2)}, u32[]{:S(2)}) collective-permute-start(f32[32,256]{1,0:T(8,128)S(1)} %get-tuple-element.23), channel_id=1, source_target_pairs={{0,16},{1,0},{2,17},{3,1},{4,18},{5,2},{6,19},{7,3},{8,20},{9,4},{... | collective-permute-start | bytes 98312 | tf_op jit(solution)/shard_map/ppermute | solution.py:143
  55.8 20.9 %collective-permute-start.4 = (bf16[16,24,512]{2,1,0:T(8,128)(2,1)S(1)}, bf16[16,24,512]{2,1,0:T(8,128)(2,1)S(1)}, u32[]{:S(2)}, u32[]{:S(2)}) collective-permute-start(bf16[16,24,512]{2,1,0:T(8,128)(2,1)S(1)} %slice.41), channel_id=1, source_target_pairs={{0,16},{1,17},{2,18},{3,19},{4,20},{5,21},{6,22},{7,23},{8,24},{9,... | collective-permute-start | bytes 1179656 | tf_op jit(solution)/shard_map/ppermute | solution.py:117
  78.9 2.7 %copy-start.1 = (bf16[96,64,512]{2,1,0:T(8,128)(2,1)}, bf16[96,64,512]{2,1,0:T(8,128)(2,1)S(1)}, u32[]{:S(2)}) copy-start(bf16[96,64,512]{2,1,0:T(8,128)(2,1)S(1)} %add_convert_fusion) | copy-start | bytes 18874372
  84.6 17.7 %all-to-all-start.2 = ((f32[16,96,128]{2,1,0:T(8,128)}), f32[16,96,128]{2,1,0:T(8,128)S(1)}, u32[]{:S(2)}, u32[]{:S(2)}) async-start(f32[16,96,128]{2,1,0:T(8,128)} %reshape.140), calls=%async_computation.2 | async-start | bytes 1572864 | tf_op jit(solution)/shard_map/all_to_all | solution.py:84
  127.9 32.8 %all-to-all-start.4 = ((bf16[16,128,512]{2,1,0:T(8,128)(2,1)}), bf16[16,128,512]{2,1,0:T(8,128)(2,1)S(1)}, u32[]{:S(2)}, u32[]{:S(2)}) async-start(bf16[16,128,512]{2,1,0:T(8,128)(2,1)} %bitcast.26), calls=%async_computation.4 | async-start | bytes 4194304 | tf_op jit(solution)/shard_map/all_to_all | solution.py:84
  167.5 6.0 %copy-start.2 = (bf16[256,8192]{1,0:T(8,128)(2,1)S(1)}, bf16[256,8192]{1,0:T(8,128)(2,1)}, u32[]{:S(2)}) copy-start(bf16[256,8192]{1,0:T(8,128)(2,1)} %param.13) | copy-start | bytes 12582916
  170.8 2.7 %collective-permute-start.5 = (f32[32,8192]{1,0:T(8,128)S(1)}, f32[32,8192]{1,0:T(8,128)S(1)}, u32[]{:S(2)}, u32[]{:S(2)}) collective-permute-start(f32[32,8192]{1,0:T(8,128)S(1)} %fusion.37), channel_id=1, source_target_pairs={{0,1},{1,0},{2,3},{3,2},{4,5},{5,4},{6,7},{7,6},{8,9},{9,8},{10,11... | collective-permute-start | bytes 3145736 | tf_op jit(solution)/shard_map/ppermute | solution.py:190
